TPU v7x, 128 devices: a whole 4x4x4 slice. The times are simulated.
128 devices in a mesh: patch: 32 (over x, z, core), grp: 4 (over y).
Axes of the slice: x: 4, y: 4, z: 4, core: 2. Of those that a mesh axis runs over, the one named last changes fastest.
Arguments:
- previous: float32 [4, 32, 12, 21, 256], P('grp', 'patch'), may hold values from -4 to 4
- predicted: float32 [4, 32, 12, 21, 256], P('grp', 'patch'), may hold values from -4 to 4
- new_owner: int32 [4, 32, 12], replicated, may hold values from 0 to 31, as said below
- levels: int32 [4, 32, 12], replicated, may hold values from 0 to 2
- diffusion: float32 [21], replicated, may hold values from 0.05 to 0.5
- decay: float32 [21], replicated, may hold values from 0.1 to 1
- reaction: float32 [21, 21], replicated, may hold values from -1.25 to 1.25
Outputs:
- solution: float32 [4, 32, 16, 21, 256], P('grp', 'patch')
Inputs may be any that keep to these rules, and one draw needn't show every extreme that they name: new_owner[b, o, s] is o, except that a patch of the last column of an owner o < 31 may get o + 1 and a patch of the first column of an owner o > 0 may get o - 1; at most 2 patches of one owner get o + 1 and at most 2 get o - 1; owner (0, 0) hands exactly 2 to o + 1 and owner (0, 31) exactly 2 to o - 1.
All inputs are finite; a program needn't handle non-finite values.
Results may differ from a plain program's by a relative error of at most 0.0003.
Values sent between devices are 32-bit elements; how exact they have to be, the bound alone decides.
No kernel may reach another device: no remote copies, remote signals or barrier semaphores. Data moves between devices by JAX's collectives and lax.ppermute only.
A program may use at most 128 MiB of HBM per device.

v0:
```python
import jax
import jax.numpy as jnp
from jax import lax
from jax.sharding import Mesh
from jax.sharding import PartitionSpec as P

SPECIES = 21
CELLS = 16
ROWS_DEV = 4
COLS_DEV = 3
MOVE_CAP = 2
KRYLOV = 3
NEWTON = 2
PATCH_DEV = 12
PATCH = ("patch_0", "patch_1", "patch_2")
PATCH_GRP = ("patch_0", "patch_1", "patch_2", "grp")
step_rate = 4.0
epsilon = 1e-12
highest = lax.Precision.HIGHEST
opposite = (1, 0, 3, 2)


def extended(x, sides, width):
    for axis, dim in sides:
        devices, length = (lax.axis_size(axis), x.shape[dim])
        up = [(i, (i + 1) % devices) for i in range(devices - 1)]
        down = [(j, i) for i, j in up]
        last = lax.slice_in_dim(x, length - width, length, axis=dim)
        initial = lax.slice_in_dim(x, 0, width, axis=dim)
        before = lax.ppermute(last, axis, up)
        after = lax.ppermute(initial, axis, down)
        x = jnp.concatenate([before, x, after], axis=dim)
    return x


def over_axes(x, axes):
    for axis in axes:
        x = lax.psum(x, axis)
    return x


def passed_along(block, axis, distance):
    devices = range(lax.axis_size(axis))
    route = [(i - distance, i) for i in devices if i - distance in devices]
    return lax.ppermute(block, axis, route)


def neighbor_ids(patch_ids, band_total, owner_total):
    valid = patch_ids >= 0
    safe = jnp.maximum(patch_ids, 0)
    per_owner = ROWS_DEV * COLS_DEV
    column_of = safe % COLS_DEV
    row_of = safe // COLS_DEV % ROWS_DEV
    owner_of = safe // per_owner % owner_total
    band_of = safe // (per_owner * owner_total)

    def compose(band_val, owner_val, row_val, column_val, inside):
        ident = ((band_val * owner_total + owner_val) * ROWS_DEV + row_val) * COLS_DEV + column_val
        return jnp.where(inside & valid, ident, -1)

    west = compose(
        band_of,
        jnp.where(column_of > 0, owner_of, owner_of - 1),
        row_of,
        jnp.where(column_of > 0, column_of - 1, COLS_DEV - 1),
        (column_of > 0) | (owner_of > 0),
    )
    east = compose(
        band_of,
        jnp.where(column_of < COLS_DEV - 1, owner_of, owner_of + 1),
        row_of,
        jnp.where(column_of < COLS_DEV - 1, column_of + 1, 0),
        (column_of < COLS_DEV - 1) | (owner_of < owner_total - 1),
    )
    south = compose(
        jnp.where(row_of > 0, band_of, band_of - 1),
        owner_of,
        jnp.where(row_of > 0, row_of - 1, ROWS_DEV - 1),
        column_of,
        (row_of > 0) | (band_of > 0),
    )
    north = compose(
        jnp.where(row_of < ROWS_DEV - 1, band_of, band_of + 1),
        owner_of,
        jnp.where(row_of < ROWS_DEV - 1, row_of + 1, 0),
        column_of,
        (row_of < ROWS_DEV - 1) | (band_of < band_total - 1),
    )
    return jnp.stack([west, east, south, north], axis=-1)


def conductance(level_vals):
    return jnp.where(level_vals == 0, 1.0, jnp.where(level_vals == 1, 4.0, 16.0)).astype(
        jnp.float32
    )


def small_solve(gram, rhs):
    dimension = gram.shape[0]
    matrix = gram
    vector = rhs
    for column_at in range(dimension):
        for target in range(column_at + 1, dimension):
            factor = matrix[target, column_at] / matrix[column_at, column_at]
            matrix = matrix.at[target].add(-factor * matrix[column_at])
            vector = vector.at[target].add(-factor * vector[column_at])
    answer = [None] * dimension
    for column_at in reversed(range(dimension)):
        running = vector[column_at]
        for later in range(column_at + 1, dimension):
            running = running - matrix[column_at, later] * answer[later]
        answer[column_at] = running / matrix[column_at, column_at]
    return jnp.stack(answer)


def pack_movers(offset, data):
    grid_off = offset.reshape(ROWS_DEV, COLS_DEV)
    row_slots = jnp.arange(ROWS_DEV, dtype=jnp.int32) * COLS_DEV
    packs = []
    for column_at, sign in ((COLS_DEV - 1, 1), (0, -1)):
        moving = (grid_off[:, column_at] == sign).astype(jnp.int32)
        ranks = jnp.cumsum(moving) - 1
        choose = (moving[:, None] == 1) & (
            ranks[:, None] == jnp.arange(MOVE_CAP, dtype=jnp.int32)[None, :]
        )
        present = jnp.any(choose, axis=0)
        source = jnp.sum(jnp.where(choose, (row_slots + column_at)[:, None], 0), axis=0)
        picked = jnp.take(data, source, axis=0)
        packs.append(jnp.where(present.reshape((MOVE_CAP,) + (1,) * (data.ndim - 1)), picked, 0.0))
    return packs


def neighbor_strips(values, window_tags, near_ids):
    slot_count = values.shape[0]
    squared = values.reshape(slot_count, SPECIES, CELLS, CELLS)
    bank = jnp.stack(
        [squared[:, :, :, 0], squared[:, :, :, -1], squared[:, :, 0, :], squared[:, :, -1, :]],
        axis=0,
    )
    flat = bank.reshape(1, 1, -1)
    half_len = flat.shape[2] // 2
    beside = extended(flat, ((PATCH, 1),), 1)
    across = extended(beside[:, :, half_len:], (("grp", 0),), 1)
    blank = jnp.zeros((1, 3, half_len), jnp.float32)
    sides = jnp.concatenate([blank, beside[:, :, :half_len], blank], axis=0)
    received = jnp.concatenate([sides, across], axis=2)
    pieces = received.reshape(9, 4, slot_count, SPECIES * CELLS)
    tags = window_tags.reshape(9 * slot_count)
    ghosts = []
    for direction in range(4):
        wanted = near_ids[:, direction]
        selector = ((wanted[:, None] == tags[None, :]) & (wanted[:, None] >= 0)).astype(jnp.float32)
        candidates = pieces[:, opposite[direction]].reshape(9 * slot_count, SPECIES * CELLS)
        picked = jnp.dot(
            selector, candidates, precision=highest, preferred_element_type=jnp.float32
        )
        ghosts.append(picked.reshape(slot_count, SPECIES, CELLS))
    return ghosts


def laplace_slots(values, ghosts, face_self, face_near):
    slot_count = values.shape[0]
    flat_pos = jnp.arange(CELLS * CELLS, dtype=jnp.int32)
    column_of = flat_pos % CELLS
    row_of = flat_pos // CELLS
    zero_one = jnp.zeros((slot_count, SPECIES, 1), jnp.float32)
    zero_row = jnp.zeros((slot_count, SPECIES, CELLS), jnp.float32)
    west_vals = jnp.where(
        column_of == 0,
        jnp.repeat(ghosts[0], CELLS, axis=-1),
        jnp.concatenate([zero_one, values[:, :, :-1]], axis=2),
    )
    east_vals = jnp.where(
        column_of == CELLS - 1,
        jnp.repeat(ghosts[1], CELLS, axis=-1),
        jnp.concatenate([values[:, :, 1:], zero_one], axis=2),
    )
    south_vals = jnp.where(
        row_of == 0,
        jnp.tile(ghosts[2], (1, 1, CELLS)),
        jnp.concatenate([zero_row, values[:, :, :-CELLS]], axis=2),
    )
    north_vals = jnp.where(
        row_of == CELLS - 1,
        jnp.tile(ghosts[3], (1, 1, CELLS)),
        jnp.concatenate([values[:, :, CELLS:], zero_row], axis=2),
    )
    own_face = face_self[:, None, None]

    def face(edge_mask, direction):
        return jnp.where(
            edge_mask,
            0.5 * (own_face + face_near[:, direction][:, None, None]),
            0.5 * (own_face + own_face),
        )

    return (
        face(column_of == 0, 0) * (west_vals - values)
        + face(column_of == CELLS - 1, 1) * (east_vals - values)
        + face(row_of == 0, 2) * (south_vals - values)
        + face(row_of == CELLS - 1, 3) * (north_vals - values)
    )


def newton_solve(
    prev_slots, pred_slots, layout_ids, band_pos, owner_pos, levels, diffusion, decay, reaction
):
    band_total, owner_total, slot_count = layout_ids.shape
    slot_ids = lax.dynamic_slice(layout_ids, (band_pos, owner_pos, 0), (1, 1, slot_count))[0, 0]
    padded_ids = jnp.pad(layout_ids, ((1, 1), (1, 1), (0, 0)), constant_values=-1)
    window_tags = lax.dynamic_slice(padded_ids, (band_pos, owner_pos, 0), (3, 3, slot_count))
    near_ids = neighbor_ids(slot_ids, band_total, owner_total)
    level_flat = levels.reshape(-1)

    def kappa_of(ident):
        return jnp.where(ident >= 0, conductance(jnp.take(level_flat, jnp.maximum(ident, 0))), 0.0)

    face_self = kappa_of(slot_ids)
    face_near = jnp.where(near_ids >= 0, kappa_of(near_ids), face_self[:, None])
    differential = (jnp.arange(SPECIES) < SPECIES - 1).astype(jnp.float32)[None, :, None]
    diff_col = diffusion[None, :, None]
    decay_col = decay[None, :, None]

    def laplace_of(values):
        return laplace_slots(
            values, neighbor_strips(values, window_tags, near_ids), face_self, face_near
        )

    def mixing(values):
        return jnp.einsum("st,kta->ksa", reaction, values, precision=highest)

    state = pred_slots
    for newton_step in range(NEWTON):
        resid = (
            differential * step_rate * (state - prev_slots)
            - diff_col * laplace_of(state)
            - mixing(state)
            + decay_col * (state * state * state)
        )
        squares = over_axes(jnp.sum(resid * resid), PATCH_GRP)
        scale = jnp.sqrt(squares + epsilon)
        basis = [-resid / scale]
        curvature = 3.0 * decay_col * (state * state)
        hess = jnp.zeros((KRYLOV + 1, KRYLOV), jnp.float32)
        for column_at in range(KRYLOV):
            current = basis[column_at]
            image = (
                differential * step_rate * current
                - diff_col * laplace_of(current)
                - mixing(current)
                + curvature * current
            )
            stacked = jnp.stack(basis)
            local_products = jnp.einsum("mksa,ksa->m", stacked, image, precision=highest)
            coeffs, length_sq = (
                over_axes(local_products, PATCH_GRP),
                over_axes(jnp.sum(image * image), PATCH_GRP),
            )
            image = image - jnp.einsum("m,mksa->ksa", coeffs, stacked, precision=highest)
            height = jnp.sqrt(length_sq - jnp.sum(coeffs * coeffs) + epsilon)
            hess = hess.at[: column_at + 1, column_at].set(coeffs)
            hess = hess.at[column_at + 1, column_at].set(height)
            basis.append(image / height)
        gram = jnp.dot(hess.T, hess, precision=highest)
        weights = small_solve(gram, scale * hess[0])
        state = state + jnp.einsum(
            "m,mksa->ksa", weights, jnp.stack(basis[:KRYLOV]), precision=highest
        )
    return state


def per_device(previous, predicted, new_owner, levels, diffusion, decay, reaction):
    band_pos = lax.axis_index("grp")
    owner_pos = lax.axis_index(PATCH)
    previous = previous[0, 0]
    predicted = predicted[0, 0]
    own_offset = (
        lax.dynamic_slice(new_owner, (band_pos, owner_pos, 0), (1, 1, PATCH_DEV))[0, 0] - owner_pos
    )
    stays = own_offset == 0
    layout_ids = jnp.arange(new_owner.size, dtype=jnp.int32).reshape(new_owner.shape)
    solved = newton_solve(
        previous, predicted, layout_ids, band_pos, owner_pos, levels, diffusion, decay, reaction
    )
    to_right, to_left = pack_movers(own_offset, solved)
    arrived = []
    for shift_by, payload in ((1, to_right), (-1, to_left)):
        arrived.append(passed_along(payload, PATCH, shift_by))
    kept = jnp.where(stays[:, None, None], solved, 0.0)
    result = jnp.concatenate([kept, arrived[0], arrived[1]], axis=0)
    return result[None, None]


def solution(mesh):
    torus = Mesh(
        mesh.devices.reshape(4, 4, 2, mesh.shape["grp"]), ("patch_0", "patch_1", "patch_2", "grp")
    )
    in_specs = (
        P("grp", PATCH, None, None, None),
        P("grp", PATCH, None, None, None),
        P(),
        P(),
        P(),
        P(),
        P(),
    )
    out_specs = P("grp", PATCH, None, None, None)
    return jax.shard_map(
        per_device, mesh=torus, in_specs=in_specs, out_specs=out_specs, check_vma=False
    )
```

profile of v0, /device:TPU:1, one launch (start us, length us, event | category | flops | bytes accessed | tf_op | source)
XLA Modules:
  0.0 771.5 jit_solution(6101554286599429304)
XLA Ops:
  57.9 9.1 %psum.392 = f32[]{:T(128)} all-reduce(f32[]{:T(128)} %get-tuple-element.531), channel_id=1, replica_groups=mesh['patch_0'=4,'patch_1'=4,'patch_2'=2,'grp'=4] {'patch_0'}, use_global_device_ids=true, to_apply=%region_1.2 | all-reduce | flops 1 | bytes 8 | tf_op jit(solution)/shard_map/psum | solution.py:38
  66.9 9.0 %psum.393 = f32[]{:T(128)} all-reduce(f32[]{:T(128)} %psum.392), channel_id=1, replica_groups=mesh['patch_0'=4,'patch_1'=4,'patch_2'=2,'grp'=4] {'patch_1'}, use_global_device_ids=true, to_apply=%region_2.3 | all-reduce | flops 1 | bytes 8 | tf_op jit(solution)/shard_map/psum | solution.py:38
  76.5 9.8 %psum.394 = f32[]{:T(128)} all-reduce(f32[]{:T(128)} %psum.393), channel_id=1, replica_groups=mesh['patch_0'=4,'patch_1'=4,'patch_2'=2,'grp'=4] {'patch_2'}, use_global_device_ids=true, to_apply=%region_3.4 | all-reduce | flops 1 | bytes 8 | tf_op jit(solution)/shard_map/psum | solution.py:38
  87.0 7.9 %psum.395 = f32[]{:T(128)} all-reduce(f32[]{:T(128)} %psum.394), channel_id=1, replica_groups=mesh['patch_0'=4,'patch_1'=4,'patch_2'=2,'grp'=4] {'grp'}, use_global_device_ids=true, to_apply=%region_4.5 | all-reduce | flops 1 | bytes 8 | tf_op jit(solution)/shard_map/psum | solution.py:38
  150.6 6.7 all-reduce.52
  157.2 11.7 %all-reduce.46 = (f32[]{:T(128)}, f32[1]{0:T(128)}) all-reduce(f32[]{:T(128)} %get-tuple-element.339, f32[1]{0:T(128)} %get-tuple-element.340), channel_id=1, replica_groups=mesh['patch_0'=4,'patch_1'=4,'patch_2'=2,'grp'=4] {'patch_1'}, use_global_device_ids=true, to_apply=%region_11.12 | all-reduce | flops 2 | bytes 16 | tf_op jit(solution)/shard_map/psum | solution.py:38
  173.7 6.9 all-reduce.40
  194.1 5.6 collective-permute-start.8
  242.8 6.8 all-reduce.51
  249.6 10.2 %all-reduce.45 = (f32[2]{0:T(128)S(1)}, f32[]{:T(128)}) all-reduce(f32[2]{0:T(128)S(1)} %get-tuple-element.337, f32[]{:T(128)} %get-tuple-element.338), channel_id=1, replica_groups=mesh['patch_0'=4,'patch_1'=4,'patch_2'=2,'grp'=4] {'patch_1'}, use_global_device_ids=true, to_apply=%region_16.17 | all-reduce | flops 3 | bytes 24 | tf_op jit(solution)/shard_map/psum | solution.py:38
  259.8 6.6 all-reduce.57
  266.4 6.7 all-reduce.39
  335.9 6.6 all-reduce.50
  342.5 9.4 %all-reduce.44 = (f32[3]{0:T(128)S(1)}, f32[]{:T(128)}) all-reduce(f32[3]{0:T(128)S(1)} %get-tuple-element.335, f32[]{:T(128)} %get-tuple-element.336), channel_id=1, replica_groups=mesh['patch_0'=4,'patch_1'=4,'patch_2'=2,'grp'=4] {'patch_1'}, use_global_device_ids=true, to_apply=%region_27.28 | all-reduce | flops 4 | bytes 32 | tf_op jit(solution)/shard_map/psum | solution.py:38
  352.0 7.7 all-reduce.56
  359.6 6.9 all-reduce.38
  436.7 6.6 psum.420
  443.9 10.6 %psum.421 = f32[]{:T(128)} all-reduce(f32[]{:T(128)} %psum.420), channel_id=1, replica_groups=mesh['patch_0'=4,'patch_1'=4,'patch_2'=2,'grp'=4] {'patch_1'}, use_global_device_ids=true, to_apply=%region_38.39 | all-reduce | flops 1 | bytes 8 | tf_op jit(solution)/shard_map/psum | solution.py:38
  455.1 5.6 psum.422
  462.3 7.2 psum.423
  525.6 6.7 all-reduce.49
  532.3 9.7 %all-reduce.43 = (f32[]{:T(128)}, f32[1]{0:T(128)}) all-reduce(f32[]{:T(128)} %get-tuple-element.333, f32[1]{0:T(128)} %get-tuple-element.334), channel_id=1, replica_groups=mesh['patch_0'=4,'patch_1'=4,'patch_2'=2,'grp'=4] {'patch_1'}, use_global_device_ids=true, to_apply=%region_47.48 | all-reduce | flops 2 | bytes 16 | tf_op jit(solution)/shard_map/psum | solution.py:38
  542.0 5.6 all-reduce.55
  547.6 6.9 all-reduce.37
  612.7 6.6 all-reduce.48
  619.3 10.6 %all-reduce.42 = (f32[2]{0:T(128)S(1)}, f32[]{:T(128)}) all-reduce(f32[2]{0:T(128)S(1)} %get-tuple-element.331, f32[]{:T(128)} %get-tuple-element.332), channel_id=1, replica_groups=mesh['patch_0'=4,'patch_1'=4,'patch_2'=2,'grp'=4] {'patch_1'}, use_global_device_ids=true, to_apply=%region_51.52 | all-reduce | flops 3 | bytes 24 | tf_op jit(solution)/shard_map/psum | solution.py:38
  629.9 6.6 all-reduce.54
  636.5 6.7 all-reduce.36
  705.3 6.6 all-reduce.47
  711.9 9.2 %all-reduce.41 = (f32[3]{0:T(128)S(1)}, f32[]{:T(128)}) all-reduce(f32[3]{0:T(128)S(1)} %get-tuple-element.329, f32[]{:T(128)} %get-tuple-element.330), channel_id=1, replica_groups=mesh['patch_0'=4,'patch_1'=4,'patch_2'=2,'grp'=4] {'patch_1'}, use_global_device_ids=true, to_apply=%region_61.62 | all-reduce | flops 4 | bytes 32 | tf_op jit(solution)/shard_map/psum | solution.py:38
  721.1 7.8 %all-reduce.53 = (f32[3]{0:T(128)S(1)}, f32[]{:T(128)}) all-reduce(f32[3]{0:T(128)S(1)} %get-tuple-element.317, f32[]{:T(128)} %get-tuple-element.318), channel_id=1, replica_groups=mesh['patch_0'=4,'patch_1'=4,'patch_2'=2,'grp'=4] {'patch_2'}, use_global_device_ids=true, to_apply=%region_62.63 | all-reduce | flops 4 | bytes 32 | tf_op jit(solution)/shard_map/psum | solution.py:38
  728.9 6.9 all-reduce.35
  (781 shorter events, 488.2 us)
Async XLA Ops:
  10.9 21.2 %collective-permute-start = (f32[1,1,16128]{2,1,0:T(1,128)S(1)}, f32[1,1,16128]{2,1,0:T(1,128)S(1)}, u32[]{:S(2)}, u32[]{:S(2)}) collective-permute-start(f32[1,1,16128]{2,1,0:T(1,128)S(1)} %reshape.2537), channel_id=1, source_target_pairs={{0,4},{4,8},{8,12},{12,16},{16,20},{20,24},{24,28},{28,32},{32,36}... | collective-permute-start | bytes 193544 | tf_op jit(solution)/shard_map/ppermute | solution.py:30
  15.8 16.3 %collective-permute-start.1 = (f32[1,1,16128]{2,1,0:T(1,128)S(1)}, f32[1,1,16128]{2,1,0:T(1,128)S(1)}, u32[]{:S(2)}, u32[]{:S(2)}) collective-permute-start(f32[1,1,16128]{2,1,0:T(1,128)S(1)} %reshape.2537), channel_id=1, source_target_pairs={{4,0},{8,4},{12,8},{16,12},{20,16},{24,20},{28,24},{32,28},{36,32}... | collective-permute-start | bytes 193544 | tf_op jit(solution)/shard_map/ppermute | solution.py:31
  35.5 5.7 collective-permute-start.3
  106.4 7.7 %collective-permute-start.4 = (f32[1,1,16128]{2,1,0:T(1,128)S(1)}, f32[1,1,16128]{2,1,0:T(1,128)S(1)}, u32[]{:S(2)}, u32[]{:S(2)}) collective-permute-start(f32[1,1,16128]{2,1,0:T(1,128)S(1)} %reshape.2544), channel_id=1, source_target_pairs={{0,4},{4,8},{8,12},{12,16},{16,20},{20,24},{24,28},{28,32},{32,36}... | collective-permute-start | bytes 193544 | tf_op jit(solution)/shard_map/ppermute | solution.py:30
  110.4 5.6 collective-permute-start.5
  118.5 5.7 collective-permute-start.7
  194.1 10.2 %collective-permute-start.8 = (f32[1,1,16128]{2,1,0:T(1,128)S(1)}, f32[1,1,16128]{2,1,0:T(1,128)S(1)}, u32[]{:S(2)}, u32[]{:S(2)}) collective-permute-start(f32[1,1,16128]{2,1,0:T(1,128)S(1)} %reshape.2554), channel_id=1, source_target_pairs={{0,4},{4,8},{8,12},{12,16},{16,20},{20,24},{24,28},{28,32},{32,36}... | collective-permute-start | bytes 193544 | tf_op jit(solution)/shard_map/ppermute | solution.py:30
  199.7 5.6 collective-permute-start.9
  205.5 5.7 collective-permute-start.10
  209.1 5.7 collective-permute-start.11
  288.8 12.8 %collective-permute-start.12 = (f32[1,1,16128]{2,1,0:T(1,128)S(1)}, f32[1,1,16128]{2,1,0:T(1,128)S(1)}, u32[]{:S(2)}, u32[]{:S(2)}) collective-permute-start(f32[1,1,16128]{2,1,0:T(1,128)S(1)} %reshape.2565), channel_id=1, source_target_pairs={{0,4},{4,8},{8,12},{12,16},{16,20},{20,24},{24,28},{28,32},{32,36}... | collective-permute-start | bytes 193544 | tf_op jit(solution)/shard_map/ppermute | solution.py:30
  294.4 7.2 collective-permute-start.13
  301.8 6.4 collective-permute-start.14
  305.5 5.7 collective-permute-start.15
  397.9 8.4 %collective-permute-start.16 = (f32[1,1,16128]{2,1,0:T(1,128)S(1)}, f32[1,1,16128]{2,1,0:T(1,128)S(1)}, u32[]{:S(2)}, u32[]{:S(2)}) collective-permute-start(f32[1,1,16128]{2,1,0:T(1,128)S(1)} %reshape.2581), channel_id=1, source_target_pairs={{0,4},{4,8},{8,12},{12,16},{16,20},{20,24},{24,28},{28,32},{32,36}... | collective-permute-start | bytes 193544 | tf_op jit(solution)/shard_map/ppermute | solution.py:30
  403.5 5.6 collective-permute-start.17
  409.3 6.1 collective-permute-start.18
  412.9 5.7 collective-permute-start.19
  481.1 9.3 %collective-permute-start.20 = (f32[1,1,16128]{2,1,0:T(1,128)S(1)}, f32[1,1,16128]{2,1,0:T(1,128)S(1)}, u32[]{:S(2)}, u32[]{:S(2)}) collective-permute-start(f32[1,1,16128]{2,1,0:T(1,128)S(1)} %reshape.2588), channel_id=1, source_target_pairs={{0,4},{4,8},{8,12},{12,16},{16,20},{20,24},{24,28},{28,32},{32,36}... | collective-permute-start | bytes 193544 | tf_op jit(solution)/shard_map/ppermute | solution.py:30
  486.7 5.6 collective-permute-start.21
  492.5 5.7 collective-permute-start.22
  496.1 5.7 collective-permute-start.23
  566.5 10.1 %collective-permute-start.24 = (f32[1,1,16128]{2,1,0:T(1,128)S(1)}, f32[1,1,16128]{2,1,0:T(1,128)S(1)}, u32[]{:S(2)}, u32[]{:S(2)}) collective-permute-start(f32[1,1,16128]{2,1,0:T(1,128)S(1)} %reshape.2598), channel_id=1, source_target_pairs={{0,4},{4,8},{8,12},{12,16},{16,20},{20,24},{24,28},{28,32},{32,36}... | collective-permute-start | bytes 193544 | tf_op jit(solution)/shard_map/ppermute | solution.py:30
  572.0 5.6 collective-permute-start.25
  577.8 5.8 collective-permute-start.26
  581.4 5.7 collective-permute-start.27
  658.3 12.8 %collective-permute-start.28 = (f32[1,1,16128]{2,1,0:T(1,128)S(1)}, f32[1,1,16128]{2,1,0:T(1,128)S(1)}, u32[]{:S(2)}, u32[]{:S(2)}) collective-permute-start(f32[1,1,16128]{2,1,0:T(1,128)S(1)} %reshape.2607), channel_id=1, source_target_pairs={{0,4},{4,8},{8,12},{12,16},{16,20},{20,24},{24,28},{28,32},{32,36}... | collective-permute-start | bytes 193544 | tf_op jit(solution)/shard_map/ppermute | solution.py:30
  663.8 7.2 collective-permute-start.29
  671.3 6.4 collective-permute-start.30
  674.9 5.7 collective-permute-start.31
  758.7 8.2 %collective-permute-start.32 = (f32[2,21,256]{2,1,0:T(8,128)S(1)}, f32[2,21,256]{2,1,0:T(8,128)S(1)}, u32[]{:S(2)}, u32[]{:S(2)}) collective-permute-start(f32[2,21,256]{2,1,0:T(8,128)S(1)} %select_select_fusion.1), channel_id=1, source_target_pairs={{0,4},{4,8},{8,12},{12,16},{16,20},{20,24},{24,28},{28,32},{32,36}... | collective-permute-start | bytes 129032 | tf_op jit(solution)/shard_map/ppermute | solution.py:45
  765.0 5.4 collective-permute-start.33
  (136 other events, 1044.7 us)
where the time goes:
time: 781 us; the launch traced here: 771 us
  blocking collectives  246 us (31%)
  local copies, waits for them, and re-layouts  231 us (30%)
  starting transfers between devices  104 us (13%)
  matrix products  69.1 us (9%)
  other arithmetic  44.7 us (6%)
  waiting for transfers between devices  39.5 us (5%)
  between operations  36 us (5%)
    psum x32, blocking collectives, over_axes(): x = lax.psum(x, axis)  246 us
    ppermute x16, starting transfers between devices, extended(): before = lax.ppermute(last, axis, up)  69.3 us
    unnamed x286, local copies, waits for them, and re-layouts  39.7 us
    ppermute x16, waiting for transfers between devices, extended(): after = lax.ppermute(initial, axis, down)  35.7 us
    ppermute x16, starting transfers between devices, extended(): after = lax.ppermute(initial, axis, down)  27.6 us
    dot_general x8, matrix products, mixing(): return jnp.einsum('st,kta->ksa', reaction, values, precision=highest)  22.3 us
    slice x8, local copies, waits for them, and re-layouts, neighbor_strips(): squared[:, :, :, 0]  21.5 us
    dot_general x64, local copies, waits for them, and re-layouts, neighbor_strips(): jnp.dot(selector, candidates, precision=highest, preferred_element_type=j...  20.5 us
  transfers between devices with their start and end apart: 34, of which 15 were waited for; matrix products, arithmetic and copies ran while one was open for 5% of the time, Pallas kernels for 0%

commit v1 on v0

--- a/solution.py
+++ b/solution.py
@@ -35,7 +35,7 @@
 
 def over_axes(x, axes):
     for axis in axes:
-        x = lax.psum(x, axis)
+        x = jnp.sum(lax.all_gather(x, axis), axis=0)
     return x
 
 

time: 781 us -> 848 us (1.086)
  local copies, waits for them, and re-layouts: 231 us -> 293 us
  blocking collectives: 246 us -> 219 us
  other arithmetic: 44.7 us -> 66.4 us
    psum x32 -> x0, blocking collectives: 246 us -> none  [over_axes(): x = lax.psum(x, axis)]
    unnamed x0 -> x32, blocking collectives: none -> 219 us
    unnamed x286 -> x398, local copies, waits for them, and re-layouts: 39.7 us -> 101 us
    reduce_sum x0 -> x56, other arithmetic: none -> 24.5 us  [over_axes(): x = jnp.sum(lax.all_gather(x, axis), axis=0)]
  transfers between devices with their start and end apart: 34 -> 34, of which waited for: 15 -> 16; matrix products, arithmetic and copies ran while one was open for 5% -> 4% of each run, Pallas kernels for 0% -> 0%
where the time goes in v1:
time: 848 us; the launch traced here: 838 us
  local copies, waits for them, and re-layouts  293 us (35%)
  blocking collectives  219 us (26%)
  starting transfers between devices  104 us (12%)
  matrix products  69 us (8%)
  other arithmetic  66.4 us (8%)
  waiting for transfers between devices  45.3 us (5%)
  between operations  41.1 us (5%)
    unnamed x32, blocking collectives  219 us
    unnamed x398, local copies, waits for them, and re-layouts  101 us
    ppermute x16, starting transfers between devices, extended(): before = lax.ppermute(last, axis, up)  69.3 us
    ppermute x16, waiting for transfers between devices, extended(): after = lax.ppermute(initial, axis, down)  41.7 us
    ppermute x16, starting transfers between devices, extended(): after = lax.ppermute(initial, axis, down)  27.4 us
    reduce_sum x56, other arithmetic, over_axes(): x = jnp.sum(lax.all_gather(x, axis), axis=0)  24.5 us
    dot_general x8, matrix products, mixing(): return jnp.einsum('st,kta->ksa', reaction, values, precision=highest)  22.1 us
    slice x8, local copies, waits for them, and re-layouts, neighbor_strips(): squared[:, :, :, 0]  20.9 us
  transfers between devices with their start and end apart: 34, of which 16 were waited for; matrix products, arithmetic and copies ran while one was open for 4% of the time, Pallas kernels for 0%

profile of v1, /device:TPU:1, one launch (start us, length us, event | category | flops | bytes accessed | tf_op | source)
XLA Modules:
  0.0 837.9 jit_solution(9398186403779580317)
XLA Ops:
  67.5 8.4 %all-reduce.35 = f32[4]{0:T(128)S(1)} all-reduce(f32[4]{0:T(128)S(1)} %dynamic-update-slice.54), channel_id=1, replica_groups=mesh['patch_0'=4,'patch_1'=4,'patch_2'=2,'grp'=4] {'patch_0'}, use_global_device_ids=true, to_apply=%add.35 | all-reduce | flops 4 | bytes 32
  78.0 8.3 all-reduce.36
  88.2 9.2 %all-reduce.37 = f32[2]{0:T(128)S(1)} all-reduce(f32[2]{0:T(128)S(1)} %dynamic-update-slice.56), channel_id=1, replica_groups=mesh['patch_0'=4,'patch_1'=4,'patch_2'=2,'grp'=4] {'patch_2'}, use_global_device_ids=true, to_apply=%add.37 | all-reduce | flops 2 | bytes 16
  99.3 7.3 all-reduce.38
  163.3 6.0 all-reduce.108
  173.3 11.0 %all-reduce.102 = (f32[4]{0:T(128)S(1)}, f32[4]{0:T(128)S(1)}) all-reduce(f32[4]{0:T(128)S(1)} %dynamic-update-slice.63, f32[4]{0:T(128)S(1)} %dynamic-update-slice.59), channel_id=1, replica_groups=mesh['patch_0'=4,'patch_1'=4,'patch_2'=2,'grp'=4] {'patch_1'}, use_global_device_ids=true, to_apply=%add.44 | all-reduce | flops 8 | bytes 64
  196.1 6.3 all-reduce.96
  217.0 5.6 collective-permute-start.8
  267.5 6.1 all-reduce.107
  276.0 9.5 %all-reduce.101 = (f32[8]{0:T(128)S(1)}, f32[4]{0:T(128)S(1)}) all-reduce(f32[8]{0:T(128)S(1)} %dynamic-update-slice.67, f32[4]{0:T(128)S(1)} %dynamic-update-slice.71), channel_id=3, replica_groups=mesh['patch_0'=4,'patch_1'=4,'patch_2'=2,'grp'=4] {'patch_1'}, use_global_device_ids=true, to_apply=%add.48 | all-reduce | flops 12 | bytes 96
  296.3 6.1 all-reduce.95
  318.6 5.5 collective-permute-start.12
  365.8 6.0 all-reduce.106
  376.2 9.1 %all-reduce.100 = (f32[12]{0:T(128)S(1)}, f32[4]{0:T(128)S(1)}) all-reduce(f32[12]{0:T(128)S(1)} %dynamic-update-slice.75, f32[4]{0:T(128)S(1)} %dynamic-update-slice.79), channel_id=7, replica_groups=mesh['patch_0'=4,'patch_1'=4,'patch_2'=2,'grp'=4] {'patch_1'}, use_global_device_ids=true, to_apply=%add.56 | all-reduce | flops 16 | bytes 128
  396.3 6.1 all-reduce.94
  434.8 5.5 collective-permute-start.16
  474.9 6.0 all-reduce.63
  482.9 9.7 %all-reduce.64 = f32[4]{0:T(128)S(1)} all-reduce(f32[4]{0:T(128)S(1)} %dynamic-update-slice.83), channel_id=1, replica_groups=mesh['patch_0'=4,'patch_1'=4,'patch_2'=2,'grp'=4] {'patch_1'}, use_global_device_ids=true, to_apply=%add.64 | all-reduce | flops 4 | bytes 32
  501.5 6.1 all-reduce.66
  519.7 5.5 collective-permute-start.20
  567.0 6.0 all-reduce.105
  577.0 9.1 %all-reduce.99 = (f32[4]{0:T(128)S(1)}, f32[4]{0:T(128)S(1)}) all-reduce(f32[4]{0:T(128)S(1)} %dynamic-update-slice.91, f32[4]{0:T(128)S(1)} %dynamic-update-slice.87), channel_id=1, replica_groups=mesh['patch_0'=4,'patch_1'=4,'patch_2'=2,'grp'=4] {'patch_1'}, use_global_device_ids=true, to_apply=%add.72 | all-reduce | flops 8 | bytes 64
  599.5 6.3 all-reduce.93
  619.1 5.5 collective-permute-start.24
  667.2 6.0 all-reduce.104
  675.6 9.7 %all-reduce.98 = (f32[8]{0:T(128)S(1)}, f32[4]{0:T(128)S(1)}) all-reduce(f32[8]{0:T(128)S(1)} %dynamic-update-slice.95, f32[4]{0:T(128)S(1)} %dynamic-update-slice.99), channel_id=11, replica_groups=mesh['patch_0'=4,'patch_1'=4,'patch_2'=2,'grp'=4] {'patch_1'}, use_global_device_ids=true, to_apply=%add.76 | all-reduce | flops 12 | bytes 96
  696.1 6.1 all-reduce.92
  717.8 5.5 collective-permute-start.28
  765.2 6.0 all-reduce.103
  775.6 9.1 %all-reduce.97 = (f32[12]{0:T(128)S(1)}, f32[4]{0:T(128)S(1)}) all-reduce(f32[12]{0:T(128)S(1)} %dynamic-update-slice.103, f32[4]{0:T(128)S(1)} %dynamic-update-slice.107), channel_id=15, replica_groups=mesh['patch_0'=4,'patch_1'=4,'patch_2'=2,'grp'=4] {'patch_1'}, use_global_device_ids=true, to_apply=%add.84 | all-reduce | flops 16 | bytes 128
  795.7 6.1 all-reduce.91
  825.1 5.5 collective-permute-start.32
  (970 shorter events, 572.6 us)
Async XLA Ops:
  10.8 29.5 %collective-permute-start = (f32[1,1,16128]{2,1,0:T(1,128)S(1)}, f32[1,1,16128]{2,1,0:T(1,128)S(1)}, u32[]{:S(2)}, u32[]{:S(2)}) collective-permute-start(f32[1,1,16128]{2,1,0:T(1,128)S(1)} %reshape.2559), channel_id=1, source_target_pairs={{0,4},{4,8},{8,12},{12,16},{16,20},{20,24},{24,28},{28,32},{32,36}... | collective-permute-start | bytes 193544 | tf_op jit(solution)/shard_map/ppermute | solution.py:30
  15.8 24.5 %collective-permute-start.1 = (f32[1,1,16128]{2,1,0:T(1,128)S(1)}, f32[1,1,16128]{2,1,0:T(1,128)S(1)}, u32[]{:S(2)}, u32[]{:S(2)}) collective-permute-start(f32[1,1,16128]{2,1,0:T(1,128)S(1)} %reshape.2559), channel_id=1, source_target_pairs={{4,0},{8,4},{12,8},{16,12},{20,16},{24,20},{28,24},{32,28},{36,32}... | collective-permute-start | bytes 193544 | tf_op jit(solution)/shard_map/ppermute | solution.py:31
  43.7 5.7 collective-permute-start.3
  118.7 6.8 collective-permute-start.4
  122.6 5.6 collective-permute-start.5
  130.8 5.7 collective-permute-start.7
  217.0 9.4 %collective-permute-start.8 = (f32[1,1,16128]{2,1,0:T(1,128)S(1)}, f32[1,1,16128]{2,1,0:T(1,128)S(1)}, u32[]{:S(2)}, u32[]{:S(2)}) collective-permute-start(f32[1,1,16128]{2,1,0:T(1,128)S(1)} %reshape.2575), channel_id=1, source_target_pairs={{0,4},{4,8},{8,12},{12,16},{16,20},{20,24},{24,28},{28,32},{32,36}... | collective-permute-start | bytes 193544 | tf_op jit(solution)/shard_map/ppermute | solution.py:30
  222.6 5.6 collective-permute-start.9
  228.4 5.7 collective-permute-start.10
  232.0 5.7 collective-permute-start.11
  318.6 9.3 %collective-permute-start.12 = (f32[1,1,16128]{2,1,0:T(1,128)S(1)}, f32[1,1,16128]{2,1,0:T(1,128)S(1)}, u32[]{:S(2)}, u32[]{:S(2)}) collective-permute-start(f32[1,1,16128]{2,1,0:T(1,128)S(1)} %reshape.2586), channel_id=1, source_target_pairs={{0,4},{4,8},{8,12},{12,16},{16,20},{20,24},{24,28},{28,32},{32,36}... | collective-permute-start | bytes 193544 | tf_op jit(solution)/shard_map/ppermute | solution.py:30
  324.1 5.6 collective-permute-start.13
  329.9 6.4 collective-permute-start.14
  333.5 5.7 collective-permute-start.15
  434.8 8.4 collective-permute-start.16
  440.3 5.6 collective-permute-start.17
  446.1 6.3 collective-permute-start.18
  449.8 5.7 collective-permute-start.19
  519.7 8.4 collective-permute-start.20
  525.2 5.6 collective-permute-start.21
  531.0 6.0 collective-permute-start.22
  534.7 5.7 collective-permute-start.23
  619.1 9.3 %collective-permute-start.24 = (f32[1,1,16128]{2,1,0:T(1,128)S(1)}, f32[1,1,16128]{2,1,0:T(1,128)S(1)}, u32[]{:S(2)}, u32[]{:S(2)}) collective-permute-start(f32[1,1,16128]{2,1,0:T(1,128)S(1)} %reshape.2618), channel_id=1, source_target_pairs={{0,4},{4,8},{8,12},{12,16},{16,20},{20,24},{24,28},{28,32},{32,36}... | collective-permute-start | bytes 193544 | tf_op jit(solution)/shard_map/ppermute | solution.py:30
  624.6 5.6 collective-permute-start.25
  630.4 5.8 collective-permute-start.26
  634.0 5.7 collective-permute-start.27
  717.8 9.3 %collective-permute-start.28 = (f32[1,1,16128]{2,1,0:T(1,128)S(1)}, f32[1,1,16128]{2,1,0:T(1,128)S(1)}, u32[]{:S(2)}, u32[]{:S(2)}) collective-permute-start(f32[1,1,16128]{2,1,0:T(1,128)S(1)} %reshape.2627), channel_id=1, source_target_pairs={{0,4},{4,8},{8,12},{12,16},{16,20},{20,24},{24,28},{28,32},{32,36}... | collective-permute-start | bytes 193544 | tf_op jit(solution)/shard_map/ppermute | solution.py:30
  723.3 5.6 collective-permute-start.29
  729.1 6.1 collective-permute-start.30
  732.8 5.7 collective-permute-start.31
  825.1 8.2 collective-permute-start.32
  831.4 5.4 collective-permute-start.33
  (137 other events, 1179.6 us)
